TPU v7x, 128 devices: a whole 4x4x4 slice. The times are simulated.
128 devices in a mesh: pod: 1, data: 64 (over z, y, x), seq: 2 (over core).
Axes of the slice: x: 4, y: 4, z: 4, core: 2. Of those that a mesh axis runs over, the one named last changes fastest.
Arguments:
- x_tokens: bfloat16 [64, 2048, 1024], P(('pod', 'data'), 'seq')
- w_query: bfloat16 [1024, 1024], replicated
- w_key: bfloat16 [1024, 1024], replicated
- w_value: bfloat16 [1024, 1024], replicated
- w_out: bfloat16 [16, 64, 1024], replicated
- dy_tokens: bfloat16 [64, 2048, 1024], P(('pod', 'data'), 'seq')
Outputs:
- output 1: bfloat16 [64, 2048, 1024], P(('pod', 'data'), 'seq')
- output 2: bfloat16 [64, 2048, 1024], P(('pod', 'data'), 'seq')
- output 3: float32 [4096, 1024], P(('pod', 'data'))
All inputs are finite; a program needn't handle non-finite values.
Results may differ from a plain program's by a relative error of at most 0.00966561.
Values are sent between devices in bfloat16 or wider.
A program may use at most 1 GiB of HBM per device.

v0:
```python
import jax
import jax.numpy as jnp
from jax import lax
from jax.sharding import PartitionSpec as P


def silu_grad(pre_act):
    sigmoid_val = jax.nn.sigmoid(pre_act)
    return sigmoid_val * (1.0 + pre_act * (1.0 - sigmoid_val))


def solution(mesh):
    seq_size = mesh.shape["seq"]
    fwd_perm = [(src_idx, src_idx + 1) for src_idx in range(seq_size - 1)]
    rev_perm = [(src_idx + 1, src_idx) for src_idx in range(seq_size - 1)]
    act_spec = P(("pod", "data"), "seq", None)
    mat_spec = P(None, None)
    out_w_spec = P(None, None, None)
    dw_spec = P(("pod", "data"), None)

    def local_layer(x_blk, w_query, w_key, w_value, w_out, dy_blk):
        num_heads, head_dim, model_dim = w_out.shape
        loc_len = x_blk.shape[1]
        blk_len = min(loc_len, 128)
        num_blk = loc_len // blk_len
        attn_scale = (head_dim * seq_size * loc_len) ** -0.5
        heads_shape = (num_blk, blk_len, num_heads, head_dim)
        flat_shape = (loc_len, model_dim)
        causal = jnp.tril(jnp.ones((blk_len, blk_len), dtype=jnp.bool_))
        wo_flat = w_out.reshape(model_dim, model_dim)
        x_loc = x_blk[0]
        dy_loc = dy_blk[0]

        q_pre = jnp.dot(x_loc, w_query, preferred_element_type=jnp.float32)
        k_pre = jnp.dot(x_loc, w_key, preferred_element_type=jnp.float32)
        v_pre = jnp.dot(x_loc, w_value, preferred_element_type=jnp.float32)
        q_feat = jax.nn.silu(q_pre).astype(jnp.bfloat16).reshape(heads_shape)
        k_feat = jax.nn.silu(k_pre).astype(jnp.bfloat16).reshape(heads_shape)
        v_feat = v_pre.astype(jnp.bfloat16).reshape(heads_shape)

        blk_states = jnp.einsum("nthk,nthv->nhkv", k_feat, v_feat, preferred_element_type=jnp.float32)
        local_state = jnp.sum(blk_states, axis=0)

        def fwd_hop(hop_index, incoming):
            return lax.ppermute(incoming + local_state, "seq", fwd_perm)

        state_in = lax.fori_loop(0, seq_size - 1, fwd_hop, jnp.zeros_like(local_state))
        prefix = (state_in[None] + jnp.cumsum(blk_states, axis=0) - blk_states).astype(jnp.bfloat16)

        scores = jnp.einsum("nthk,nshk->nhts", q_feat, k_feat, preferred_element_type=jnp.float32)
        masked = jnp.where(causal, scores, 0.0).astype(jnp.bfloat16)
        intra_part = jnp.einsum("nhts,nshv->nthv", masked, v_feat, preferred_element_type=jnp.float32)
        inter_part = jnp.einsum("nthk,nhkv->nthv", q_feat, prefix, preferred_element_type=jnp.float32)
        attn_out = (attn_scale * (intra_part + inter_part)).astype(jnp.bfloat16).reshape(flat_shape)
        y_loc = jnp.dot(attn_out, wo_flat, preferred_element_type=jnp.float32).astype(jnp.bfloat16)

        d_attn = jnp.einsum("te,de->td", dy_loc, wo_flat, preferred_element_type=jnp.float32).astype(jnp.bfloat16).reshape(heads_shape)
        rev_blocks = jnp.einsum("nthk,nthv->nhkv", q_feat, d_attn, preferred_element_type=jnp.float32)
        local_rev = jnp.sum(rev_blocks, axis=0)

        def rev_hop(hop_index, incoming):
            return lax.ppermute(incoming + local_rev, "seq", rev_perm)

        rev_in = lax.fori_loop(0, seq_size - 1, rev_hop, jnp.zeros_like(local_rev))
        suffix = (rev_in[None] + local_rev[None] - jnp.cumsum(rev_blocks, axis=0)).astype(jnp.bfloat16)

        dv_scores = jnp.where(causal, jnp.einsum("nthv,nshv->nhts", d_attn, v_feat, preferred_element_type=jnp.float32), 0.0).astype(jnp.bfloat16)
        dq_val = (jnp.einsum("nhts,nshk->nthk", dv_scores, k_feat, preferred_element_type=jnp.float32)
                  + jnp.einsum("nthv,nhkv->nthk", d_attn, prefix, preferred_element_type=jnp.float32))
        dk_val = (jnp.einsum("nhts,nthk->nshk", dv_scores, q_feat, preferred_element_type=jnp.float32)
                  + jnp.einsum("nshv,nhkv->nshk", v_feat, suffix, preferred_element_type=jnp.float32))
        dv_val = (jnp.einsum("nhts,nthv->nshv", masked, d_attn, preferred_element_type=jnp.float32)
                  + jnp.einsum("nshk,nhkv->nshv", k_feat, suffix, preferred_element_type=jnp.float32))
        grad_q = (attn_scale * dq_val.reshape(flat_shape) * silu_grad(q_pre)).astype(jnp.bfloat16)
        grad_k = (attn_scale * dk_val.reshape(flat_shape) * silu_grad(k_pre)).astype(jnp.bfloat16)
        grad_v = (attn_scale * dv_val.reshape(flat_shape)).astype(jnp.bfloat16)

        dx_loc = (jnp.einsum("te,de->td", grad_q, w_query, preferred_element_type=jnp.float32)
                  + jnp.einsum("te,de->td", grad_k, w_key, preferred_element_type=jnp.float32)
                  + jnp.einsum("te,de->td", grad_v, w_value, preferred_element_type=jnp.float32)).astype(jnp.bfloat16)
        dw_local = jnp.concatenate([
            jnp.einsum("td,te->de", x_loc, grad_q, preferred_element_type=jnp.float32),
            jnp.einsum("td,te->de", x_loc, grad_k, preferred_element_type=jnp.float32),
            jnp.einsum("td,te->de", x_loc, grad_v, preferred_element_type=jnp.float32),
            jnp.einsum("td,te->de", attn_out, dy_loc, preferred_element_type=jnp.float32),
        ], axis=0)
        dw_part = lax.psum_scatter(dw_local, "data", scatter_dimension=0, tiled=True)
        dw_part = lax.psum(dw_part, "seq")
        return y_loc[None], dx_loc[None], dw_part

    return jax.shard_map(local_layer, mesh=mesh,
                         in_specs=(act_spec, mat_spec, mat_spec, mat_spec, out_w_spec, act_spec),
                         out_specs=(act_spec, act_spec, dw_spec), check_vma=False)
```

profile of v0, /device:TPU:1, one launch (start us, length us, event | category | flops | bytes accessed | tf_op | source)
XLA Modules:
  0.0 630.0 jit_solution(8457113096400879228)
XLA Ops:
  7.2 0.0 reduce-scatter.2.cloned.1.call-start
  7.2 6.1 fusion.23
  13.3 6.4 %reshape.49 = bf16[8,128,16,64]{3,2,1,0:T(8,128)(2,1)} reshape(bf16[1024,1024]{1,0:T(8,128)(2,1)} %fusion.23) | data formatting | bytes 4194304 | tf_op jit(solution)/shard_map/reshape | solution.py:57
  19.6 5.8 copy.41
  25.5 6.9 %multiply_convert_fusion.5 = (bf16[1024,1024]{1,0:T(8,128)(2,1)}, f32[1024,1024]{1,0:T(8,128)}) fusion(bf16[1024,1024]{1,0:T(8,128)(2,1)} %param.7, bf16[1,1024,1024]{2,1,0:T(8,128)(2,1)S(1)} %copy-done), kind=kOutput, calls=%fused_computation.14 | convolution fusion | flops 2152726528 | bytes 10485760 | tf_op jit(solution)/shard_map/dot_general | solution.py:34
  32.4 6.4 %reshape.47 = bf16[8,128,16,64]{3,2,1,0:T(8,128)(2,1)} reshape(bf16[1024,1024]{1,0:T(8,128)(2,1)} %get-tuple-element.20) | data formatting | bytes 4194304 | tf_op jit(solution)/shard_map/reshape | solution.py:37
  38.8 5.8 copy.32
  44.5 5.5 fusion.34
  50.1 4.1 collective-permute-start.1
  54.2 3.7 fusion.20
  57.8 6.6 %reshape.46 = bf16[8,128,16,64]{3,2,1,0:T(8,128)(2,1)} reshape(bf16[1024,1024]{1,0:T(8,128)(2,1)} %fusion.20) | data formatting | bytes 4194304 | tf_op jit(solution)/shard_map/reshape | solution.py:39
  64.4 5.8 copy.34
  70.2 6.0 fusion.14
  76.2 1.5 select_convert_fusion
  77.7 0.1 copy-done.1
  77.8 1.2 fusion.40
  79.1 0.9 copy-done.8
  80.0 1.6 copy-done.12
  81.5 5.3 fusion.36
  86.9 1.5 add.68
  88.4 0.4 copy-done.9
  88.8 3.1 multiply_bitcast_fusion
  91.8 7.2 %copy.60 = f32[8,128,16,64]{3,2,1,0:T(8,128)} copy(f32[8,128,16,64]{1,3,2,0:T(8,128)} %multiply_bitcast_fusion) | data formatting | bytes 8388608 | tf_op jit(solution)/shard_map/mul | solution.py:75
  99.0 7.6 %reshape.45 = f32[1024,1024]{1,0:T(8,128)} reshape(f32[8,128,16,64]{3,2,1,0:T(8,128)} %copy.60) | data formatting | bytes 8388608 | tf_op jit(solution)/shard_map/mul | solution.py:75
  106.6 5.7 multiply_convert_fusion.1
  112.3 6.4 %reshape.48 = bf16[8,128,16,64]{3,2,1,0:T(8,128)(2,1)} reshape(bf16[1024,1024]{1,0:T(8,128)(2,1)} %get-tuple-element.19) | data formatting | bytes 4194304 | tf_op jit(solution)/shard_map/reshape | solution.py:38
  118.7 6.2 copy.33
  124.9 7.9 %fusion.38 = f32[8,16,64,128]{3,2,1,0:T(8,128)} fusion(bf16[8,128,16,64]{1,3,2,0:T(8,128)(2,1)} %copy.33, bf16[8,16,128,128]{3,2,1,0:T(8,128)(2,1)} %copy-done.8), kind=kOutput, calls=%fused_computation.53 | convolution fusion | flops 268435456 | bytes 10485760 | tf_op jit(solution)/shard_map/nhts,nshk->nthk/dot_general | solution.py:68
  132.8 1.5 select_convert_fusion.1
  134.3 0.1 copy-done.7
  134.3 1.3 fusion.35
  135.6 0.3 copy-done.4
  135.9 3.2 fusion.41
  139.1 3.5 fusion.33
  142.7 1.8 copy.56
  144.5 1.5 collective-permute-start
  145.9 4.3 convolution_bitcast_fusion
  150.3 4.4 convolution_bitcast_fusion.1
  154.6 3.1 fusion.37
  157.7 0.7 subtract_convert_fusion.1
  158.4 1.0 fusion.32
  159.5 1.1 copy-done.11
  160.6 2.8 multiply_bitcast_fusion.1
  163.4 1.8 copy.39
  165.2 1.3 copy-done.19
  166.5 4.5 fusion.4
  171.0 7.2 %copy.59 = f32[8,128,16,64]{3,2,1,0:T(8,128)} copy(f32[8,128,16,64]{1,3,2,0:T(8,128)} %multiply_bitcast_fusion.1) | data formatting | bytes 8388608 | tf_op jit(solution)/shard_map/mul | solution.py:74
  178.2 7.6 %reshape.44 = f32[1024,1024]{1,0:T(8,128)} reshape(f32[8,128,16,64]{3,2,1,0:T(8,128)} %copy.59) | data formatting | bytes 8388608 | tf_op jit(solution)/shard_map/mul | solution.py:74
  185.8 4.9 multiply_convert_fusion.2
  190.7 1.3 copy-done.16
  192.0 2.4 convolution_bitcast_fusion.2
  194.5 1.0 copy-done.14
  195.5 1.2 copy-done.15
  196.7 7.1 %pad_maximum_fusion = f32[4096,1024]{1,0:T(8,128)} fusion(f32[1024,1024]{1,0:T(8,128)S(1)} %copy-done.15, f32[1024,1024]{1,0:T(8,128)S(1)} %copy-done.13, f32[1024,1024]{1,0:T(8,128)S(1)} %copy-done.14, f32[1024,1024]{1,0:T(8,128)S(1)} %convolution_bitcast_fusion.2), kind=kLoop, calls=%fused_computation | loop fusion | flops 12582912 | bytes 33554432 | tf_op jit(solution)/shard_map/concatenate | solution.py:81
  203.8 0.0 reduce-scatter.2.cloned.1.call-update
  203.8 0.0 all-reduce.2.cloned.1.call-start
  203.9 4.8 fusion.2
  208.7 2.4 fusion.39
  211.1 3.7 fusion
  214.8 337.2 %reduce-scatter.2.cloned.1.call-done = f32[64,1024]{1,0:T(8,128)} async-done(((f32[4096,1024]{1,0:T(8,128)}), f32[64,1024]{1,0:T(8,128)}) %reduce-scatter.2.cloned.1.call-update) | async-done | bytes 262160 | tf_op jit(solution)/shard_map/reduce_scatter | solution.py:87
  552.0 0.0 all-reduce.2.cloned.1.call-update
  552.0 5.9 convert_bitcast_fusion
  558.0 63.2 %all-reduce.2.cloned.1.call-done = f32[64,1024]{1,0:T(8,128)} async-done(((f32[64,1024]{1,0:T(8,128)}), f32[64,1024]{1,0:T(8,128)}) %all-reduce.2.cloned.1.call-update) | async-done | bytes 262160 | tf_op jit(solution)/shard_map/psum | solution.py:88
  621.1 1.7 copy.90
  (44 shorter events, 0.1 us)
Async XLA Ops:
  7.2 18.3 %copy-start = (bf16[1,1024,1024]{2,1,0:T(8,128)(2,1)S(1)}, bf16[1,1024,1024]{2,1,0:T(8,128)(2,1)}, u32[]{:S(2)}) copy-start(bf16[1,1024,1024]{2,1,0:T(8,128)(2,1)} %param.6) | copy-start | bytes 6291460
  7.2 544.8 %reduce-scatter.2.cloned.1.call-start = ((), (), s32[]{:S(2)}) async-start(), calls=%async_computation.1 | async-start | bytes 17039360 | tf_op jit(solution)/shard_map/reduce_scatter | solution.py:87
  44.5 9.6 %copy-start.23 = (bf16[1024,1024]{1,0:T(8,128)(2,1)S(1)}, bf16[1024,1024]{1,0:T(8,128)(2,1)}, u32[]{:S(2)}) copy-start(bf16[1024,1024]{1,0:T(8,128)(2,1)} %param.9) | copy-start | bytes 6291460
  50.1 36.8 %collective-permute-start.1 = (f32[16,64,64]{2,1,0:T(8,128)S(1)}, f32[16,64,64]{2,1,0:T(8,128)}, u32[]{:S(2)}, u32[]{:S(2)}) collective-permute-start(f32[16,64,64]{2,1,0:T(8,128)S(1)} %get-tuple-element.25), channel_id=1, source_target_pairs={{1,0},{3,2},{5,4},{7,6},{9,8},{11,10},{13,12},{15,14},{17,16},{19,... | collective-permute-start | bytes 786440 | tf_op jit(solution)/shard_map/while/body/eval_jaxpr/ppermute | solution.py:62
  70.2 6.1 copy-start.3
  70.2 6.1 copy-start.6
  76.2 1.6 copy-start.1
  77.8 2.1 copy-start.8
  77.8 3.7 copy-start.12
  86.9 1.9 copy-start.9
  124.8 7.9 %copy-start.2 = (bf16[8,128,16,64]{1,3,2,0:T(8,128)(2,1)S(1)}, bf16[8,128,16,64]{1,3,2,0:T(8,128)(2,1)}, u32[]{:S(2)}) copy-start(bf16[8,128,16,64]{1,3,2,0:T(8,128)(2,1)} %copy.32) | copy-start | bytes 6291460
  124.8 7.9 %copy-start.5 = (bf16[8,128,16,64]{1,3,2,0:T(8,128)(2,1)S(1)}, bf16[8,128,16,64]{1,3,2,0:T(8,128)(2,1)}, u32[]{:S(2)}) copy-start(bf16[8,128,16,64]{1,3,2,0:T(8,128)(2,1)} %copy.33) | copy-start | bytes 6291460
  132.8 1.6 copy-start.7
  134.3 1.6 copy-start.4
  135.9 3.2 copy-start.10
  144.4 5.8 copy-start.18
  144.5 13.2 %collective-permute-start = (f32[16,64,64]{2,1,0:T(8,128)S(1)}, f32[16,64,64]{2,1,0:T(8,128)S(1)}, u32[]{:S(2)}, u32[]{:S(2)}) collective-permute-start(f32[16,64,64]{2,1,0:T(8,128)S(1)} %get-tuple-element.27), channel_id=1, source_target_pairs={{0,1},{2,3},{4,5},{6,7},{8,9},{10,11},{12,13},{14,15},{16,17},{18,... | collective-permute-start | bytes 786440 | tf_op jit(solution)/shard_map/while/body/eval_jaxpr/ppermute | solution.py:45
  145.9 4.3 copy-start.20
  158.4 2.2 copy-start.11
  163.4 3.1 copy-start.22
  165.2 1.3 copy-start.19
  190.7 1.3 copy-start.16
  192.0 2.4 copy-start.13
  192.0 3.5 copy-start.14
  192.0 4.7 copy-start.15
  203.8 417.3 %all-reduce.2.cloned.1.call-start = ((), (), s32[]{:S(2)}) async-start(), calls=%async_computation.2 | async-start | bytes 524288 | tf_op jit(solution)/shard_map/psum | solution.py:88
  203.9 4.8 copy-start.17
  203.9 4.8 copy-start.24
  208.7 2.4 copy-start.21
  208.7 2.4 copy-start.25
Sparse Core Ops, SparseCore 0:
  203.9 348.0 reduce-scatter.1
  554.4 66.6 all-reduce.1
where the time goes:
time: 639 us; the launch traced here: 630 us
  waiting for transfers between devices  400 us (63%)
  local copies, waits for them, and re-layouts  93.4 us (15%)
  matrix products  90.7 us (14%)
  other arithmetic  25.2 us (4%)
  between operations  14.7 us (2%)
    reduce_scatter x1, waiting for transfers between devices, local_layer(): lax.psum_scatter(dw_local, 'data', scatter_dimension=0, tiled=True)  337 us
    psum x1, waiting for transfers between devices, local_layer(): dw_part = lax.psum(dw_part, 'seq')  63.2 us
    mul x2, local copies, waits for them, and re-layouts, local_layer(): attn_scale * dq_val.reshape(flat_shape) * silu_grad(q_pre)  14.8 us
    mul x2, local copies, waits for them, and re-layouts, local_layer(): attn_scale * dk_val.reshape(flat_shape) * silu_grad(k_pre)  14.8 us
  transfers between devices with their start and end apart: 4, of which 2 were waited for; matrix products, arithmetic and copies ran while one was open for 9% of the time, Pallas kernels for 0%

commit v1 on v0

v1 whole, which is shorter than its diff:
```python
import jax
import jax.numpy as jnp
from jax import lax
from jax.experimental import pallas as pl
from jax.experimental.pallas import tpu as pltpu
from jax.sharding import PartitionSpec as P

MESH = pl.DeviceIdType.MESH
F32 = jnp.float32
BF16 = jnp.bfloat16

TOK = 1024
SEQ = 2 * TOK
DIM = 1024
HALF = DIM // 2
GRP = 256
CHUNK = 256
NCH = SEQ // CHUNK
BLK = 512
ROWS = 64

ORDER = (("z", "y", "x"), ("y", "x", "z"), ("x", "z", "y"))
PART_ROWS = ((0, 16), (16, 24), (40, 24))
AXES = ("z", "y", "x")


def dot(a, b):
    return lax.dot_general(a, b, (((1,), (0,)), ((), ())), preferred_element_type=F32)


def dot_t(a, b):
    return lax.dot_general(a, b, (((1,), (1,)), ((), ())), preferred_element_type=F32)


def t_dot(a, b):
    return lax.dot_general(a, b, (((0,), (0,)), ((), ())), preferred_element_type=F32)


class Ids:
    def __init__(self):
        self.n = 0

    def take(self):
        self.n += 1
        return self.n - 1


NUM_SEMS = 128
NUM_LOCAL = 16


def kernel(scale, x_hbm, dy_hbm, wq_hbm, wk_hbm, wv_hbm, wo_hbm,
           y_hbm, dx_hbm, dw_ref,
           xf, xt, dyf, wq, wk, wv, wo, sga, sgb, qg, kg, vg, dog,
           pre, pre_t, suf, suf_t, state, oo, o_in, gq, gk, gv, g_in, acc, fin,
           r00, l00, m00, r01, l01, m01, r02, l02, m02,
           r10, l10, m10, r11, l11, m11, r12, l12, m12,
           r20, l20, m20, r21, l21, m21, r22, l22, m22,
           send_sem, recv_sem, local_sem):
    core = lax.axis_index("seq")
    data = lax.axis_index("data")
    me = {"z": data // 16, "y": (data // 4) % 4, "x": data % 4}
    other = 1 - core
    hop_bufs = {(0, 0): (r00, l00, m00), (0, 1): (r01, l01, m01), (0, 2): (r02, l02, m02),
                (1, 0): (r10, l10, m10), (1, 1): (r11, l11, m11), (1, 2): (r12, l12, m12),
                (2, 0): (r20, l20, m20), (2, 1): (r21, l21, m21), (2, 2): (r22, l22, m22)}
    ids = Ids()
    sent = []

    def device(axis, delta):
        c = dict(me)
        c[axis] = (c[axis] + delta + 4) % 4
        return {"data": (c["z"] * 4 + c["y"]) * 4 + c["x"], "seq": core}

    partner = {"data": data, "seq": other}

    def remote(src, dst, dev):
        k = ids.take()
        return pltpu.make_async_remote_copy(src_ref=src, dst_ref=dst, send_sem=send_sem.at[k],
                                            recv_sem=recv_sem.at[k], device_id=dev, device_id_type=MESH)

    def start(copy):
        copy.start()
        sent.append(copy)

    def acc_slice(part, phase, g, h, j, m=None):
        r0, nr = PART_ROWS[part]
        where = {}
        for p, axis in enumerate(ORDER[part]):
            where[axis] = me[axis] if p < phase else j if p == phase else slice(None)
        if m is not None:
            where["z"] = m
        return acc.at[(g, h, where["z"], where["y"], where["x"], pl.ds(r0, nr), slice(None))]

    def buf_slice(buf, part, phase, g, h, m=None):
        rest = [a for a in AXES if a in ORDER[part][phase + 1:]]
        idx = [h, g] + [m if (a == "z" and m is not None) else slice(None) for a in rest]
        return buf.at[tuple(idx)]

    def hop_copies(part, phase, g, m=None):
        axis = ORDER[part][phase]
        i = me[axis]
        from_opp, from_left, from_right = hop_bufs[part, phase]
        c_opp, c_r, c_l = (i + 2) % 4, (i + 1) % 4, (i + 3) % 4
        right, left = device(axis, 1), device(axis, -1)
        mk = lambda h, j, buf, dev: remote(acc_slice(part, phase, g, h, j, m), buf_slice(buf, part, phase, g, h, m), dev)
        return {
            "1A": mk(0, c_opp, from_opp, right), "1B": mk(1, c_opp, from_opp, left),
            "RB": mk(1, c_r, from_left, right), "LA": mk(0, c_l, from_right, left),
            "RA": mk(0, c_r, from_left, right), "LB": mk(1, c_l, from_right, left),
            "key": (part, phase, g, m),
        }

    def hop_start(c):
        for k in ("1A", "1B", "RB", "LA"):
            start(c[k])

    def add_into(part, phase, g, m, h, j, bufs):
        rest = [a for a in AXES if a in ORDER[part][phase + 1:]]
        r0, nr = PART_ROWS[part]
        g_list = [g] if isinstance(g, int) else list(range(2))
        m_list = ([m] if isinstance(m, int) else list(range(4)) if m is None else list(range(3)))
        for gi in g_list:
            grid = [()]
            for a in rest:
                vals = m_list if a == "z" else range(4)
                grid = [t + (v,) for t in grid for v in vals]
            for t in grid:
                where = {}
                for p, axis in enumerate(ORDER[part]):
                    where[axis] = me[axis] if p < phase else j if p == phase else t[rest.index(axis)]
                at = (gi, h, where["z"], where["y"], where["x"], pl.ds(r0, nr), slice(None))
                total = acc[at]
                for b in bufs:
                    total = total + b[(h, gi) + t + (slice(None), slice(None))]
                acc[at] = total

    def hop_relay(c):
        part, phase, g, m = c["key"]
        i = me[ORDER[part][phase]]
        from_opp, _, _ = hop_bufs[part, phase]
        c["1A"].wait_recv()
        add_into(part, phase, g, m, 0, (i + 1) % 4, [from_opp])
        start(c["RA"])
        c["1B"].wait_recv()
        add_into(part, phase, g, m, 1, (i + 3) % 4, [from_opp])
        start(c["LB"])

    def hop_finish(c):
        part, phase, g, m = c["key"]
        i = me[ORDER[part][phase]]
        _, from_left, from_right = hop_bufs[part, phase]
        for k in ("RB", "LA", "RA", "LB"):
            c[k].wait_recv()
        for h in range(2):
            add_into(part, phase, g, m, h, i, [from_left, from_right])

    both = slice(None)
    low = pl.ds(0, 3)
    E = [{p: hop_copies(p, 0, g, low) for p in (1, 2)} for g in range(2)]
    L = {p: hop_copies(p, 0, both, 3) for p in (1, 2)}
    Z = hop_copies(0, 0, both)
    P2 = {p: hop_copies(p, 1, both) for p in range(3)}
    P3 = {p: hop_copies(p, 2, both) for p in range(3)}

    own0 = pl.multiple_of(core * TOK, TOK)
    oth0 = pl.multiple_of(other * TOK, TOK)
    loads = {}
    for k, (name, src, dst) in enumerate([
            ("x", x_hbm, xf.at[pl.ds(own0, TOK)]), ("wq", wq_hbm, wq), ("wk", wk_hbm, wk), ("wv", wv_hbm, wv),
            ("wo", wo_hbm, wo), ("dy", dy_hbm, dyf.at[pl.ds(own0, TOK)])]):
        loads[name] = pltpu.make_async_copy(src, dst, local_sem.at[k])
        loads[name].start()
    barrier = pltpu.get_barrier_semaphore()
    for dev in [partner] + [device(a, s) for a in AXES for s in (1, -1)]:
        pl.semaphore_signal(barrier, inc=1, device_id=dev, device_id_type=MESH)
    pl.semaphore_wait(barrier, 7)
    x_send = remote(x_hbm, xf.at[pl.ds(own0, TOK)], partner)
    dy_send = remote(dy_hbm, dyf.at[pl.ds(own0, TOK)], partner)
    start(x_send)
    start(dy_send)

    lanes = lax.broadcasted_iota(jnp.int32, (1, 128), 1)
    first = (lanes < 64).astype(F32).astype(BF16)
    second = (lanes >= 64).astype(F32).astype(BF16)
    causal = (lax.broadcasted_iota(jnp.int32, (CHUNK, CHUNK), 0)
              >= lax.broadcasted_iota(jnp.int32, (CHUNK, CHUNK), 1))
    block_diag = ((lax.broadcasted_iota(jnp.int32, (128, 128), 0) < 64)
                  == (lax.broadcasted_iota(jnp.int32, (128, 128), 1) < 64))

    def project(g, base0):
        off = pl.multiple_of(core * HALF + g * GRP, GRP)

        def body(i, _):
            base = pl.multiple_of(base0 + i * BLK, BLK)
            rows = pl.ds(base, BLK)
            xa = xf[rows, :]
            if g == 0:
                xt[:, rows] = xa.T
            for w, sg, out in ((wq, sga, qg), (wk, sgb, kg)):
                a = dot(xa, w[:, pl.ds(off, GRP)])
                s = jax.nn.sigmoid(a)
                out[rows, :] = (a * s).astype(BF16)
                sg[rows, :] = s * (1.0 + a * (1.0 - s))
            vg[rows, :] = dot(xa, wv[:, pl.ds(off, GRP)]).astype(BF16)
            dog[rows, :] = dot_t(dyf[rows, :], wo[pl.ds(off, GRP), :]).astype(BF16)
            return 0

        lax.fori_loop(0, TOK // BLK, body, 0)

    def scan_states():
        for a_ref, b_ref, out, out_t, order in ((kg, vg, pre, pre_t, 1), (qg, dog, suf, suf_t, -1)):
            for j in range(2):
                state[j] = jnp.zeros((128, 128), F32)

            def body(n, _):
                i = n if order == 1 else NCH - 1 - n
                rows = pl.ds(pl.multiple_of(i * CHUNK, CHUNK), CHUNK)
                for j in range(2):
                    cols = pl.ds(j * 128, 128)
                    st = state[j]
                    stb = st.astype(BF16)
                    out[i, j] = stb
                    out_t[i, j] = stb.T
                    kv = t_dot(a_ref[rows, cols], b_ref[rows, cols])
                    state[j] = st + jnp.where(block_diag, kv, 0.0)
                return 0

            lax.fori_loop(0, NCH, body, 0)

    def attend(g):
        def body(i, _):
            rows = pl.ds(pl.multiple_of(i * CHUNK, CHUNK), CHUNK)
            for j in range(2):
                cols = pl.ds(j * 128, 128)
                ocols = pl.ds(g * GRP + j * 128, 128)
                q, k, v, do = qg[rows, cols], kg[rows, cols], vg[rows, cols], dog[rows, cols]
                qa, qb, ka, kb = q * first, q * second, k * first, k * second
                va, vb, da, db = v * first, v * second, do * first, do * second
                p_a = jnp.where(causal, dot_t(qa, k), 0.0).astype(BF16)
                p_b = jnp.where(causal, dot_t(qb, k), 0.0).astype(BF16)
                d_a = jnp.where(causal, dot_t(da, v), 0.0).astype(BF16)
                d_b = jnp.where(causal, dot_t(db, v), 0.0).astype(BF16)
                o = dot(p_a, va) + dot(p_b, vb) + dot(q, pre[i, j])
                oo[rows, ocols] = (scale * o).astype(BF16)
                dq = dot(d_a, ka) + dot(d_b, kb) + dot(do, pre_t[i, j])
                gq[rows, ocols] = (scale * dq * sga[rows, cols]).astype(BF16)
                dk = t_dot(d_a, qa) + t_dot(d_b, qb) + dot(v, suf_t[i, j])
                gk[rows, ocols] = (scale * dk * sgb[rows, cols]).astype(BF16)
                dv = t_dot(p_a, da) + t_dot(p_b, db) + dot(k, suf[i, j])
                gv[rows, ocols] = (scale * dv).astype(BF16)
            return 0

        lax.fori_loop(0, NCH, body, 0)

    def weight_grads(g):
        cols = pl.ds(g * GRP, GRP)
        for m, gr in enumerate((gq, gk, gv)):
            def body(n, _):
                lhs = xt[pl.ds(pl.multiple_of(n * 512, 512), 512), :]
                t = dot(lhs, gr[:, cols])
                for h in range(2):
                    for yy in range(2):
                        for xx in range(4):
                            r = yy * 256 + xx * 64
                            acc[g, h, m, n * 2 + yy, xx] = t[r:r + 64, h * 128:h * 128 + 128]
                return 0

            lax.fori_loop(0, 2, body, 0)

    o_sends, g_sends = [], []
    for g in range(2):
        cols = pl.ds(g * GRP, GRP)
        if g == 0:
            for name in ("x", "wq", "wk", "wv", "wo", "dy"):
                loads[name].wait()
        project(g, core * TOK)
        if g == 0:
            x_send.wait_recv()
            dy_send.wait_recv()
        project(g, other * TOK)
        scan_states()
        if g == 1:
            for p in (1, 2):
                hop_relay(E[0][p])
        attend(g)
        o_sends.append(remote(oo.at[:, cols], o_in.at[:, cols], partner))
        start(o_sends[-1])
        for m, gr in enumerate((gq, gk, gv)):
            g_sends.append(remote(gr.at[pl.ds(oth0, TOK), cols], g_in.at[m, :, cols], partner))
            start(g_sends[-1])
        if g == 1:
            for p in (1, 2):
                hop_finish(E[0][p])
        weight_grads(g)
        for p in (1, 2):
            hop_start(E[g][p])

    for s in o_sends:
        s.wait_recv()

    def dwo(src, first_row_block):
        def body(n, _):
            lhs = src[:, pl.ds(pl.multiple_of(n * 256, 256), 256)]
            t = t_dot(lhs, dyf[:, pl.ds(pl.multiple_of(core * HALF, HALF), HALF)])
            for g in range(2):
                for h in range(2):
                    for xx in range(4):
                        acc[g, h, 3, first_row_block + n, xx] = t[xx * 64:xx * 64 + 64, g * 256 + h * 128:g * 256 + h * 128 + 128]
            return 0

        lax.fori_loop(0, 2, body, 0)

    dwo(oo, core * 2)
    dwo(o_in, other * 2)
    hop_start(Z)
    for p in (1, 2):
        hop_start(L[p])

    own_c = pl.ds(pl.multiple_of(core * HALF, HALF), HALF)
    oth_c = pl.ds(pl.multiple_of(other * HALF, HALF), HALF)

    def y_body(n, _):
        rows = pl.ds(pl.multiple_of(own0 + n * 512, 512), 512)
        t = dot(oo[rows, :], wo[own_c, :]) + dot(o_in[rows, :], wo[oth_c, :])
        xf[pl.ds(pl.multiple_of(n * 512, 512), 512), :] = t.astype(BF16)
        return 0

    def dx_body(n, _):
        rows = pl.ds(pl.multiple_of(own0 + n * 512, 512), 512)
        r = pl.ds(pl.multiple_of(n * 512, 512), 512)
        t = None
        for m, (gr, w) in enumerate(((gq, wq), (gk, wk), (gv, wv))):
            u = dot_t(gr[rows, :], w[:, own_c]) + dot_t(g_in[m, r, :], w[:, oth_c])
            t = u if t is None else t + u
        xf[pl.ds(pl.multiple_of(TOK + n * 512, 512), 512), :] = t.astype(BF16)
        return 0

    lax.fori_loop(0, 2, y_body, 0)
    y_out = pltpu.make_async_copy(xf.at[pl.ds(0, TOK)], y_hbm, local_sem.at[6])
    y_out.start()
    for p in (1, 2):
        hop_relay(E[1][p])
    hop_relay(Z)
    for p in (1, 2):
        hop_relay(L[p])
    for s in g_sends:
        s.wait_recv()
    lax.fori_loop(0, 2, dx_body, 0)
    dx_out = pltpu.make_async_copy(xf.at[pl.ds(TOK, TOK)], dx_hbm, local_sem.at[7])
    dx_out.start()

    for p in (1, 2):
        hop_finish(E[1][p])
        hop_finish(L[p])
        hop_start(P2[p])
    hop_finish(Z)
    hop_start(P2[0])
    for p in (1, 2, 0):
        hop_relay(P2[p])
    for p in (1, 2, 0):
        hop_finish(P2[p])
        hop_start(P3[p])
    for p in (1, 2, 0):
        hop_relay(P3[p])
    for p in (1, 2, 0):
        hop_finish(P3[p])

    final = acc.at[:, :, me["z"], me["y"], me["x"]]
    last = remote(final, fin, partner)
    start(last)
    for g in range(2):
        for h in range(2):
            at = pl.ds(pl.multiple_of(core * HALF + g * 256 + h * 128, 128), 128)
            dw_ref[:, at] = acc[g, h, me["z"], me["y"], me["x"]]
    last.wait_recv()
    for g in range(2):
        for h in range(2):
            at = pl.ds(pl.multiple_of(other * HALF + g * 256 + h * 128, 128), 128)
            dw_ref[:, at] = fin[g, h]
    for s in sent:
        s.wait_send()
    y_out.wait()
    dx_out.wait()
    assert ids.n <= NUM_SEMS, ids.n


def hop_shapes(part, phase):
    rest = len(ORDER[part]) - phase - 1
    shape = (2, 2) + (4,) * rest + (PART_ROWS[part][1], 128)
    return [pltpu.VMEM(shape, F32)] * 3


def solution(mesh):
    act = P(("pod", "data"), "seq", None)
    scale = float((64 * SEQ) ** -0.5)

    def local(x, wq, wk, wv, wo, dy):
        vm = pltpu.VMEM
        any_ = pl.BlockSpec(memory_space=pl.ANY)
        scratch = [
            vm((SEQ, DIM), BF16), vm((DIM, SEQ), BF16), vm((SEQ, DIM), BF16),
            *[vm((DIM, DIM), BF16)] * 4,
            *[vm((SEQ, GRP), F32)] * 2, *[vm((SEQ, GRP), BF16)] * 4,
            *[vm((NCH, 2, 128, 128), BF16)] * 4, vm((2, 128, 128), F32),
            vm((SEQ, HALF), BF16), vm((SEQ, HALF), BF16), *[vm((SEQ, HALF), BF16)] * 3, vm((3, TOK, HALF), BF16),
            vm((2, 2, 4, 4, 4, ROWS, 128), F32), vm((2, 2, ROWS, 128), F32),
        ]
        for part in range(3):
            for phase in range(3):
                scratch += hop_shapes(part, phase)
        scratch += [pltpu.SemaphoreType.DMA((NUM_SEMS,)), pltpu.SemaphoreType.DMA((NUM_SEMS,)),
                    pltpu.SemaphoreType.DMA((NUM_LOCAL,))]
        y, dx, dw = pl.pallas_call(
            lambda *refs: kernel(scale, *refs),
            out_shape=(jax.ShapeDtypeStruct((TOK, DIM), BF16), jax.ShapeDtypeStruct((TOK, DIM), BF16),
                       jax.ShapeDtypeStruct((ROWS, DIM), F32)),
            in_specs=[any_] * 6,
            out_specs=(any_, any_, pl.BlockSpec(memory_space=pltpu.VMEM)),
            scratch_shapes=scratch,
            name="layer",
            compiler_params=pltpu.CompilerParams(collective_id=0, has_side_effects=True, vmem_limit_bytes=67043328),
        )(x[0], dy[0], wq, wk, wv, wo.reshape(DIM, DIM))
        return y[None], dx[None], dw

    return jax.shard_map(local, mesh=mesh,
                         in_specs=(act, P(None, None), P(None, None), P(None, None), P(None, None, None), act),
                         out_specs=(act, act, P(("pod", "data"), None)), check_vma=False)
```

time: 639 us -> 103 us (0.16); the launches traced: 630 us -> 103 us
  waiting for transfers between devices: 400 us -> 0 us
  Pallas kernels: 0 us -> 97.4 us
  matrix products: 90.7 us -> 0 us
  local copies, waits for them, and re-layouts: 93.4 us -> 5.26 us
  other arithmetic: 25.2 us -> 0 us
  between operations: 14.7 us -> 0.65 us
    reduce_scatter x1 -> x0, waiting for transfers between devices: 337 us -> none  [local_layer(): lax.psum_scatter(dw_local, 'data', scatter_dimension=0, tiled=True)]
    pallas_call x0 -> x1, Pallas kernels: none -> 97.4 us  [local(): pl.pallas_call(lambda *refs: kernel(scale, *refs), out_shape=(jax.ShapeDt...]
    dot_general x24 -> x0, matrix products: 90.7 us -> none  [the longest x1 7.89 us: local_layer(): jnp.einsum('nhts,nshk->nthk', dv_scores, k_feat, preferred_element_type=j...]
    psum x1 -> x0, waiting for transfers between devices: 63.2 us -> none  [local_layer(): dw_part = lax.psum(dw_part, 'seq')]
    reshape x8 -> x0, local copies, waits for them, and re-layouts: 49.2 us -> none  [the longest x2 12.5 us: local_layer(): k_feat = jax.nn.silu(k_pre).astype(jnp.bfloat16).reshape(heads_shape)]
    mul x4 -> x0, local copies, waits for them, and re-layouts: 29.6 us -> none  [the longest x2 14.8 us: local_layer(): attn_scale * dq_val.reshape(flat_shape) * silu_grad(q_pre)]
    convert_element_type x2 -> x0, other arithmetic: 10.6 us -> none  [the longest x1 5.66 us: local_layer(): (attn_scale * dk_val.reshape(flat_shape) * silu_grad(k_pre)).astype(jnp.b...]
    concatenate x1 -> x0, other arithmetic: 7.09 us -> none  [local_layer(): jnp.concatenate([jnp.einsum('td,te->de', x_loc, grad_q, preferred_element...]
  transfers between devices with their start and end apart: 4 -> 0, of which waited for: 2 -> 0; matrix products, arithmetic and copies ran while one was open for 9% -> 0% of each run, Pallas kernels for 0% -> 0%
where the time goes in v1:
time: 103 us
  Pallas kernels  97.4 us (95%)
  local copies, waits for them, and re-layouts  5.26 us (5%)
    pallas_call x1, Pallas kernels, local(): pl.pallas_call(lambda *refs: kernel(scale, *refs), out_shape=(jax.ShapeDt...  97.4 us
    unnamed x7, local copies, waits for them, and re-layouts  5.26 us

profile of v1, /device:TPU:1, one launch (start us, length us, event | category | flops | bytes accessed | tf_op | source)
XLA Modules:
  0.0 103.3 jit_solution(18436230331634709582)
XLA Ops:
  0.6 97.4 %layer.1 = (bf16[1024,1024]{1,0:T(8,128)(2,1)}, bf16[1024,1024]{1,0:T(8,128)(2,1)}, f32[64,1024]{1,0:T(8,128)}) custom-call(bf16[1024,1024]{1,0:T(8,128)(2,1)} %bitcast.7, bf16[1024,1024]{1,0:T(8,128)(2,1)} %bitcast.8, bf16[1024,1024]{1,0:T(8,128)(2,1)} %refs_2_.1, bf16[1024,1024]{1,0:T(8,128)(2,1)} %refs_3_.1, bf16[1024,1024]{1,0:T(8,128)(2,1)} %refs_4_.1, ...), custom_call_target="tpu_custom_call" | custom-call | tf_op jit(solution)/shard_map/layer/pallas_call | solution.py:414
  98.1 0.0 copy-start
  98.1 3.2 %copy.12 = bf16[1,1024,1024]{2,1,0:T(8,128)(2,1)} copy(bf16[1,1024,1024]{2,1,0:T(8,128)(2,1)} %bitcast.6) | data formatting | bytes 4194304
  101.3 0.0 copy-done
  101.3 0.0 copy-start.1
  101.3 1.3 %copy.13 = bf16[1,1024,1024]{2,1,0:T(8,128)(2,1)} copy(bf16[1,1024,1024]{2,1,0:T(8,128)(2,1)S(1)} %bitcast.5) | data formatting | bytes 4194304
  102.6 0.0 copy-done.1
  102.6 0.7 copy.14
Async XLA Ops:
  98.1 3.2 %copy-start = (bf16[1024,1024]{1,0:T(8,128)(2,1)S(1)}, bf16[1024,1024]{1,0:T(8,128)(2,1)}, u32[]{:S(2)}) copy-start(bf16[1024,1024]{1,0:T(8,128)(2,1)} %get-tuple-element.7) | copy-start | bytes 6291460
  101.3 1.3 %copy-start.1 = (f32[64,1024]{1,0:T(8,128)S(1)}, f32[64,1024]{1,0:T(8,128)}, u32[]{:S(2)}) copy-start(f32[64,1024]{1,0:T(8,128)} %get-tuple-element.14) | copy-start | bytes 786436

commit v2 on v0

v2 whole, which is shorter than its diff:
```python
import jax
import jax.numpy as jnp
from jax import lax
from jax.experimental import pallas as pl
from jax.experimental.pallas import tpu as pltpu
from jax.sharding import PartitionSpec as P

MESH = pl.DeviceIdType.MESH
F32 = jnp.float32
BF16 = jnp.bfloat16

TOK = 1024
SEQ = 2 * TOK
DIM = 1024
HALF = DIM // 2
GRP = 256
CHUNK = 256
NCH = SEQ // CHUNK
BLK = 512
ROWS = 64

ORDER = (("z", "y", "x"), ("y", "x", "z"), ("x", "z", "y"))
PART_ROWS = ((0, 16), (16, 24), (40, 24))
AXES = ("z", "y", "x")


def dot(a, b):
    return lax.dot_general(a, b, (((1,), (0,)), ((), ())), preferred_element_type=F32)


def dot_t(a, b):
    return lax.dot_general(a, b, (((1,), (1,)), ((), ())), preferred_element_type=F32)


def t_dot(a, b):
    return lax.dot_general(a, b, (((0,), (0,)), ((), ())), preferred_element_type=F32)


NUM_SEMS = 240
NUM_LOCAL = 12
KINDS = {"1A": (0, 2, 0, 1), "1B": (1, 2, 0, -1), "RB": (1, 1, 1, 1), "LA": (0, 3, 2, -1),
         "RA": (0, 1, 1, 1), "LB": (1, 3, 2, -1),
         "O": (slice(None), 2, 0, 2), "R": (slice(None), 1, 1, 1), "L": (slice(None), 3, 2, -1)}
RAW = ("1A", "1B", "RB", "LA")
RING = ("RB", "LA", "RA", "LB")
LAST = ("O", "R", "L")
GENS = {"E0": (0, 0, 3, None), "L0": (None, 3, 1, 0), "E1": (1, 0, 3, None), "L1": (None, 3, 1, 1)}


def when(cond, fn):
    if cond is None:
        fn()
    else:
        pl.when(cond)(fn)


def both(a, b):
    return b if a is None else a if b is None else jnp.logical_and(a, b)


def kernel(scale, x_hbm, dy_hbm, wq_hbm, wk_hbm, wv_hbm, wo_hbm,
           y_ref, dx_ref, dw_ref,
           xf, xt, dyf, wq, wk, wv, wo, sga, sgb, qg, kg, vg,
           kv_raw, qd_raw, oo, o_in, gq, gk, gv, g_in, acc, fin,
           r00, l00, m00, r01, l01, m01, r02, l02, m02,
           r10, l10, m10, r11, l11, m11, r12, l12, m12,
           r20, l20, m20, r21, l21, m21, r22, l22, m22,
           send_sem, recv_sem, local_sem):
    core = lax.axis_index("seq")
    data = lax.axis_index("data")
    me = {"z": lax.div(data, 16), "y": lax.rem(lax.div(data, 4), 4), "x": lax.rem(data, 4)}
    at = {a: [me[a]] + [lax.rem(me[a] + k, 4) for k in (1, 2, 3)] for a in AXES}
    yat = [lax.rem(v, 2) * 2 + lax.div(v, 2) for v in at["y"]]
    stride = {"z": 16, "y": 4, "x": 1}
    away = {a: [data + (at[a][k] - me[a]) * stride[a] for k in range(4)] for a in AXES}
    is_last = [v == 3 for v in at["z"]]
    not_last = [v != 3 for v in at["z"]]
    parity = [[lax.rem(v, 2) == par for v in at["y"]] for par in (0, 1)]
    conds = {}
    other = 1 - core
    hop_bufs = {(0, 0): (r00, l00, m00), (0, 1): (r01, l01, m01), (0, 2): (r02, l02, m02),
                (1, 0): (r10, l10, m10), (1, 1): (r11, l11, m11), (1, 2): (r12, l12, m12),
                (2, 0): (r20, l20, m20), (2, 1): (r21, l21, m21), (2, 2): (r22, l22, m22)}
    sem_ids = {}
    sent = []

    def device(axis, delta):
        return {"data": away[axis][delta % 4], "seq": core}

    partner = {"data": data, "seq": other}

    def remote(name, src, dst, dev):
        k = sem_ids.setdefault(name, len(sem_ids))
        assert k < NUM_SEMS
        return pltpu.make_async_remote_copy(src_ref=src, dst_ref=dst, send_sem=send_sem.at[k],
                                            recv_sem=recv_sem.at[k], device_id=dev, device_id_type=MESH)

    def start(copy):
        copy.start()
        sent.append((copy, None))

    def gen_test(gen, axis, k):
        _, m_lo, _, par = GENS[gen]
        if axis == "z":
            return ("z", m_lo != 0, k)
        if axis == "y" and par is not None:
            return ("y", par, k)
        return None

    def active(gen, part, phase, step):
        tests = [gen_test(gen, axis, 0 if p < phase else step) for p, axis in enumerate(ORDER[part][:phase + 1])]
        key = tuple(sorted(t for t in tests if t is not None))
        if key not in conds:
            cond = None
            for axis, kind, k in key:
                cond = both(cond, (is_last if kind else not_last)[k] if axis == "z" else parity[kind][k])
            conds[key] = cond
        return conds[key]

    def place(part, phase, step):
        where = {}
        for p, a in enumerate(ORDER[part][:phase + 1]):
            k = 0 if p < phase else step
            where[a] = yat[k] if a == "y" else at[a][k]
        return where

    def free_range(gen, axis, msub=None):
        _, m_lo, mn, par = GENS[gen]
        if axis == "z":
            return (m_lo, mn) if msub is None else (msub, 1)
        if axis == "y" and par is not None:
            return 2 * par, 2
        return 0, 4

    def copy_of(gen, part, phase, kind, msub=None):
        h, step, b, direction = KINDS[kind]
        g = GENS[gen][0]
        gsl = pl.ds(0, 2) if g is None else pl.ds(g, 1)
        row0, nr = PART_ROWS[part]
        where, land = place(part, phase, step), [gsl, h]
        for a in AXES:
            if a not in where:
                where[a] = pl.ds(*free_range(gen, a, msub))
                land.append(where[a])
        src = acc.at[(gsl, h, where["z"], where["y"], where["x"], pl.ds(row0, nr), slice(None))]
        return remote((gen, part, phase, kind), src, hop_bufs[part, phase][b].at[tuple(land)],
                      device(ORDER[part][phase], direction))

    def send(gen, part, phase, kind):
        cond = active(gen, part, phase, KINDS[kind][1])
        copy = copy_of(gen, part, phase, kind)
        when(cond, copy.start)
        sent.append((copy, cond))

    def ring_start(gen, kinds, m=None):
        last = m is None or m == 2
        for kind in kinds:
            for part in (1, 2, 0):
                step = KINDS[kind][1]
                cond = active(gen, part, 0, step)
                if ORDER[part][0] == "z":
                    copy = copy_of(gen, part, 0, kind)
                    when(at["z"][step] == (3 if m is None else m), copy.start)
                else:
                    copy = copy_of(gen, part, 0, kind, m)
                    when(cond, copy.start)
                if last:
                    sent.append((copy_of(gen, part, 0, kind), cond))

    def add_into(gen, part, phase, hs, step, bufs):
        row0, nr = PART_ROWS[part]
        g = GENS[gen][0]
        where, land = place(part, phase, step), []
        for a in AXES:
            if a not in where:
                where[a] = pl.ds(*free_range(gen, a))
                land.append(where[a])
        for gi in ((0, 1) if g is None else (g,)):
            for h in hs:
                spot = (gi, h, where["z"], where["y"], where["x"], pl.ds(row0, nr), slice(None))
                total = acc[spot]
                for b in bufs:
                    total = total + b[(gi, h, *land, slice(None), slice(None))]
                acc[spot] = total

    def relay(gens, phase, parts=(1, 2, 0)):
        for part in parts:
            for gen in gens:
                for got, out in (("1A", "RA"), ("1B", "LB")):
                    step = KINDS[out][1]
                    cond = active(gen, part, phase, step)
                    arrived = copy_of(gen, part, phase, got)
                    copy = copy_of(gen, part, phase, out)

                    def go():
                        arrived.wait_recv()
                        add_into(gen, part, phase, (KINDS[out][0],), step, [hop_bufs[part, phase][0]])
                        copy.start()

                    when(cond, go)
                    sent.append((copy, cond))

    def finish(gens, phase, parts=(1, 2, 0)):
        for part in parts:
            for gen in gens:
                arrivals = [copy_of(gen, part, phase, k) for k in (LAST if phase == 2 else RING)]

                def go():
                    for a in arrivals:
                        a.wait_recv()
                    add_into(gen, part, phase, (0, 1), 0, list(hop_bufs[part, phase][0 if phase == 2 else 1:]))

                when(active(gen, part, phase, 0), go)
                if phase < 2:
                    for kind in (RAW if phase == 0 else LAST):
                        send(gen, part, phase + 1, kind)

    def wait_sends(copies):
        for copy, cond in copies:
            when(cond, copy.wait_send)
        copies.clear()

    own0 = pl.multiple_of(core * TOK, TOK)
    oth0 = pl.multiple_of(other * TOK, TOK)
    barrier = pltpu.get_barrier_semaphore()
    for dev in [partner] + [device(a, s) for a in AXES for s in (1, -1)]:
        pl.semaphore_signal(barrier, inc=1, device_id=dev, device_id_type=MESH)
    own_c = pl.ds(pl.multiple_of(core * HALF, HALF), HALF)
    oth_c = pl.ds(pl.multiple_of(other * HALF, HALF), HALF)
    loads = {}

    def load(name, src, dst):
        loads[name] = pltpu.make_async_copy(src, dst, local_sem.at[len(loads)])
        loads[name].start()

    load("x", x_hbm, xf.at[pl.ds(own0, TOK)])
    for name, src, dst in (("wq", wq_hbm, wq), ("wk", wk_hbm, wk), ("wv", wv_hbm, wv)):
        load(name, src.at[:, own_c], dst)
    load("dy", dy_hbm, dyf.at[pl.ds(own0, TOK)])
    load("wo", wo_hbm.at[own_c], wo)

    lanes = lax.broadcasted_iota(jnp.int32, (1, 128), 1)
    first = (lanes < 64).astype(F32).astype(BF16)
    second = (lanes >= 64).astype(F32).astype(BF16)
    causal = (lax.broadcasted_iota(jnp.int32, (CHUNK, CHUNK), 0)
              >= lax.broadcasted_iota(jnp.int32, (CHUNK, CHUNK), 1))
    block_diag = ((lax.broadcasted_iota(jnp.int32, (128, 128), 0) < 64)
                  == (lax.broadcasted_iota(jnp.int32, (128, 128), 1) < 64))

    def chunk_products(a, b, raw, base, blk):
        for n in range(blk // CHUNK):
            rs = slice(n * CHUNK, (n + 1) * CHUNK)
            p = t_dot(a[rs, :], b[rs, :])
            for j in range(2):
                cs = slice(j * 128, j * 128 + 128)
                raw[lax.div(base, CHUNK) + n, j] = p[cs, cs]

    def project_x(g, base, blk):
        rows = pl.ds(base, blk)
        gcols = pl.ds(g * GRP, GRP)
        xa = xf[rows, :]
        if g == 0:
            xt[:, rows] = xa.T
        kept = []
        for w, sg, out in ((wq, sga, qg), (wk, sgb, kg)):
            a = dot(xa, w[:, gcols])
            s = pl.reciprocal(1.0 + jnp.exp(-a))
            kept.append((a * s).astype(BF16))
            out[rows, :] = kept[-1]
            sg[rows, :] = s * (1.0 + a * (1.0 - s))
        v = dot(xa, wv[:, gcols]).astype(BF16)
        vg[rows, :] = v
        chunk_products(kept[1], v, kv_raw, base, blk)

    def project_dy(g, half, base):
        rows = pl.ds(base, TOK)
        do = dot_t(dyf[rows, :], wo[pl.ds(g * GRP, GRP), :]).astype(BF16)
        dx_ref[:, pl.ds(pl.multiple_of(half * GRP, GRP), GRP)] = do
        chunk_products(qg[rows, :], do, qd_raw, base, TOK)

    def scan_states():
        for raw, side, order in ((kv_raw, 0, range(NCH)), (qd_raw, 1, range(NCH - 1, -1, -1))):
            for j in range(2):
                st = jnp.zeros((128, 128), F32)
                for i in order:
                    y_ref[i * 128:i * 128 + 128, (side * 2 + j) * 128:(side * 2 + j) * 128 + 128] = st.astype(BF16)
                    st = st + jnp.where(block_diag, raw[i, j], 0.0)

    def attend(g, lo, hi):
        def body(i, _):
            rows = pl.ds(pl.multiple_of(i * CHUNK, CHUNK), CHUNK)
            srows = pl.ds(pl.multiple_of(i * 128, 128), 128)
            drows = pl.ds(pl.multiple_of(lax.rem(i, 4) * CHUNK, CHUNK), CHUNK)
            for j in range(2):
                cols = pl.ds(j * 128, 128)
                pre, suf = y_ref[srows, cols], y_ref[srows, pl.ds(256 + j * 128, 128)]
                ocols = pl.ds(g * GRP + j * 128, 128)
                q, k, v = qg[rows, cols], kg[rows, cols], vg[rows, cols]
                do = dx_ref[drows, pl.ds(pl.multiple_of(lax.div(i, 4) * GRP + j * 128, 128), 128)]
                qa, qb, ka, kb = q * first, q * second, k * first, k * second
                va, vb, da, db = v * first, v * second, do * first, do * second
                p_a = jnp.where(causal, dot_t(qa, k), 0.0).astype(BF16)
                p_b = jnp.where(causal, dot_t(qb, k), 0.0).astype(BF16)
                d_a = jnp.where(causal, dot_t(da, v), 0.0).astype(BF16)
                d_b = jnp.where(causal, dot_t(db, v), 0.0).astype(BF16)
                o = dot(p_a, va) + dot(p_b, vb) + dot(q, pre)
                oo[rows, ocols] = (scale * o).astype(BF16)
                dq = dot(d_a, ka) + dot(d_b, kb) + dot_t(do, pre)
                gq[rows, ocols] = (scale * dq * sga[rows, cols]).astype(BF16)
                dk = t_dot(d_a, qa) + t_dot(d_b, qb) + dot_t(v, suf)
                gk[rows, ocols] = (scale * dk * sgb[rows, cols]).astype(BF16)
                dv = t_dot(p_a, da) + t_dot(p_b, db) + dot(k, suf)
                gv[rows, ocols] = (scale * dv).astype(BF16)
            return 0

        lax.fori_loop(lo, hi, body, 0)

    def weight_grad(g, m):
        gr = (gq, gk, gv)[m]

        for n in range(2):
            t = dot(xt[n * 512:n * 512 + 512, :], gr[:, pl.ds(g * GRP, GRP)])
            for h in range(2):
                for yy in range(2):
                    for xx in range(4):
                        r = yy * 256 + xx * 64
                        acc[g, h, m, yy * 2 + n, xx] = t[r:r + 64, h * 128:h * 128 + 128]

    def out_weight_grad(g):
        rhs_cols = pl.ds(pl.multiple_of(core * HALF, HALF), HALF)
        for src, who in ((oo, core), (o_in, other)):
            t = t_dot(src[:, pl.ds(g * GRP, GRP)], dyf[:, rhs_cols])
            for gg in range(2):
                for h in range(2):
                    for xx in range(4):
                        c0 = gg * 256 + h * 128
                        acc[gg, h, 3, g * 2 + who, xx] = t[xx * 64:xx * 64 + 64, c0:c0 + 128]

    def share(g):
        cols = pl.ds(g * GRP, GRP)
        o_copy = remote(("o", g), oo.at[:, cols], o_in.at[:, cols], partner)
        start(o_copy)
        g_copies = []
        for m, gr in enumerate((gq, gk, gv)):
            g_copies.append(remote(("g", g, m), gr.at[pl.ds(oth0, TOK), cols], g_in.at[m, :, cols], partner))
            start(g_copies[-1])
        return o_copy, g_copies

    a0 = core * TOK
    with jax.named_scope("load0"):
        for name in ("x", "wq", "wk", "wv"):
            loads[name].wait()
    project_x(0, pl.multiple_of(a0, BLK), BLK)
    with jax.named_scope("barrier"):
        pl.semaphore_wait(barrier, 7)
    x_send = remote("x", x_hbm, xf.at[pl.ds(own0, TOK)], partner)
    dy_send = remote("dy", dy_hbm, dyf.at[pl.ds(own0, TOK)], partner)
    start(x_send)
    start(dy_send)
    with jax.named_scope("projA0"):
        project_x(0, pl.multiple_of(a0 + BLK, BLK), BLK)
        for name in ("dy", "wo"):
            loads[name].wait()
        project_dy(0, core, own0)
    with jax.named_scope("xrecv"):
        x_send.wait_recv()
    with jax.named_scope("projB0"):
        for n in range(2):
            project_x(0, pl.multiple_of(oth0 + n * BLK, BLK), BLK)
    with jax.named_scope("dyrecv"):
        dy_send.wait_recv()
    with jax.named_scope("projBd0"):
        project_dy(0, other, oth0)
    with jax.named_scope("scan0"):
        scan_states()
    with jax.named_scope("attend0"):
        attend(0, 0, NCH)
    o_copy0, g_copies0 = share(0)
    with jax.named_scope("wgrad0"):
        for m in range(3):
            weight_grad(0, m)
            ring_start("E0", ("1A", "1B"), m)
    with jax.named_scope("dwo0"):
        o_copy0.wait_recv()
        out_weight_grad(0)
        ring_start("L0", ("1A", "1B"))
        for m in range(3):
            ring_start("E0", ("RB", "LA"), m)
        ring_start("L0", ("RB", "LA"))

    with jax.named_scope("projA1"):
        for n in range(2):
            project_x(1, pl.multiple_of(own0 + n * BLK, BLK), BLK)
        project_dy(1, core, own0)
    with jax.named_scope("r1E0"):
        relay(("E0",), 0)
    with jax.named_scope("projB1a"):
        for n in range(2):
            project_x(1, pl.multiple_of(oth0 + n * BLK, BLK), BLK)
    with jax.named_scope("r1L0"):
        relay(("L0",), 0)
    with jax.named_scope("projB1b"):
        project_dy(1, other, oth0)
    load("wq2", wq_hbm.at[:, oth_c], xf.at[pl.ds(0, DIM), pl.ds(0, HALF)])
    load("wk2", wk_hbm.at[:, oth_c], xf.at[pl.ds(0, DIM), pl.ds(HALF, HALF)])
    load("wv2", wv_hbm.at[:, oth_c], xf.at[pl.ds(DIM, DIM), pl.ds(0, HALF)])
    for n in range(2):
        load(f"wo2{n}", wo_hbm.at[oth_c, pl.ds(n * HALF, HALF)], xf.at[pl.ds(DIM + n * HALF, HALF), pl.ds(HALF, HALF)])
    with jax.named_scope("scan1"):
        scan_states()
    with jax.named_scope("attend1a"):
        attend(1, 0, 3)
    with jax.named_scope("f1_0"):
        finish(("E0", "L0"), 0)
    with jax.named_scope("attend1b"):
        attend(1, 3, 7)
    with jax.named_scope("r2_0"):
        relay(("E0", "L0"), 1)
    with jax.named_scope("attend1c"):
        attend(1, 7, 8)
    o_copy1, g_copies1 = share(1)
    with jax.named_scope("wgrad1"):
        for m in range(3):
            weight_grad(1, m)
            ring_start("E1", ("1A", "1B"), m)
            if m == 1:
                with jax.named_scope("f2_0"):
                    finish(("E0", "L0"), 1)
    with jax.named_scope("dwo1"):
        o_copy1.wait_recv()
        out_weight_grad(1)
        ring_start("L1", ("1A", "1B"))
        for m in range(3):
            ring_start("E1", ("RB", "LA"), m)
        ring_start("L1", ("RB", "LA"))

    def y_part(r, n):
        rows, cols = pl.ds(pl.multiple_of(own0 + r * HALF, HALF), HALF), pl.ds(n * HALF, HALF)
        t = dot(oo[rows, :], wo[:, cols]) + dot(o_in[rows, :], xf[pl.ds(DIM + n * HALF, HALF), pl.ds(HALF, HALF)])
        y_ref[pl.ds(r * HALF, HALF), cols] = t.astype(BF16)

    def dx_part(r, n):
        rows, cols = pl.ds(pl.multiple_of(own0 + r * HALF, HALF), HALF), pl.ds(n * HALF, HALF)
        t = None
        for m, (gr, w, w2) in enumerate(((gq, wq, xf.at[cols, pl.ds(0, HALF)]), (gk, wk, xf.at[cols, pl.ds(HALF, HALF)]),
                                         (gv, wv, xf.at[pl.ds(DIM + n * HALF, HALF), pl.ds(0, HALF)]))):
            u = dot_t(gr[rows, :], w[cols, :]) + dot_t(g_in[m, pl.ds(r * HALF, HALF), :], w2[...])
            t = u if t is None else t + u
        dx_ref[pl.ds(r * HALF, HALF), cols] = t.astype(BF16)

    for name in ("wq2", "wk2", "wv2", "wo20", "wo21"):
        loads[name].wait()
    with jax.named_scope("Y"):
        for r in range(2):
            for n in range(2):
                y_part(r, n)
    for c in g_copies0 + g_copies1:
        c.wait_recv()
    with jax.named_scope("dX0"):
        dx_part(0, 0)
    with jax.named_scope("r1E1"):
        relay(("E1", "L1"), 0)
    with jax.named_scope("dX1"):
        dx_part(0, 1)
    with jax.named_scope("f3_0"):
        finish(("E0", "L0"), 2)
    with jax.named_scope("dX2"):
        dx_part(1, 0)
    with jax.named_scope("dX3"):
        dx_part(1, 1)
    last_gens = ("E1", "L1")
    with jax.named_scope("f1_1"):
        finish(last_gens, 0)
    with jax.named_scope("sends"):
        early = sent[:-36]
        del sent[:-36]
        wait_sends(early)
    with jax.named_scope("r2_1"):
        relay(last_gens, 1)
    with jax.named_scope("f2_1"):
        finish(last_gens, 1)
    with jax.named_scope("f3_1"):
        finish(last_gens, 2)

    final = acc.at[:, :, me["z"], yat[0], me["x"]]
    last = remote("final", final, fin, partner)
    start(last)
    with jax.named_scope("sends2"):
        for g in range(2):
            for h in range(2):
                cols = pl.ds(pl.multiple_of(core * HALF + g * 256 + h * 128, 128), 128)
                dw_ref[:, cols] = acc[g, h, me["z"], yat[0], me["x"]]
        wait_sends(sent)
    with jax.named_scope("last"):
        last.wait_recv()
    for g in range(2):
        for h in range(2):
            cols = pl.ds(pl.multiple_of(other * HALF + g * 256 + h * 128, 128), 128)
            dw_ref[:, cols] = fin[g, h]
    wait_sends(sent)


def hop_shapes(part, phase):
    rest = 2 - phase
    return [pltpu.VMEM((2, 2) + (4,) * rest + (PART_ROWS[part][1], 128), F32)] * 3


def solution(mesh):
    act = P(("pod", "data"), "seq", None)
    scale = float((64 * SEQ) ** -0.5)

    def local(x, wq, wk, wv, wo, dy):
        vm = pltpu.VMEM
        any_ = pl.BlockSpec(memory_space=pl.ANY)
        scratch = [
            vm((SEQ, DIM), BF16), vm((DIM, SEQ), BF16), vm((SEQ, DIM), BF16),
            *[vm((DIM, HALF), BF16)] * 3, vm((HALF, DIM), BF16),
            *[vm((SEQ, GRP), F32)] * 2, *[vm((SEQ, GRP), BF16)] * 3,
            *[vm((NCH, 2, 128, 128), F32)] * 2,
            vm((SEQ, HALF), BF16), vm((SEQ, HALF), BF16), *[vm((SEQ, HALF), BF16)] * 3, vm((3, TOK, HALF), BF16),
            vm((2, 2, 4, 4, 4, ROWS, 128), F32), vm((2, 2, ROWS, 128), F32),
        ]
        for part in range(3):
            for phase in range(3):
                scratch += hop_shapes(part, phase)
        scratch += [pltpu.SemaphoreType.DMA((NUM_SEMS,)), pltpu.SemaphoreType.DMA((NUM_SEMS,)),
                    pltpu.SemaphoreType.DMA((NUM_LOCAL,))]
        y, dx, dw = pl.pallas_call(
            lambda *refs: kernel(scale, *refs),
            out_shape=(vm((TOK, DIM), BF16), vm((TOK, DIM), BF16), vm((ROWS, DIM), F32)),
            in_specs=[any_] * 6,
            out_specs=(pl.BlockSpec(memory_space=pltpu.VMEM),) * 3,
            scratch_shapes=scratch,
            name="layer",
            compiler_params=pltpu.CompilerParams(collective_id=0, has_side_effects=True, vmem_limit_bytes=62560000),
        )(x[0], dy[0], wq, wk, wv, wo.reshape(DIM, DIM))
        return y[None], dx[None], dw

    return jax.shard_map(local, mesh=mesh,
                         in_specs=(act, P(None, None), P(None, None), P(None, None), P(None, None, None), act),
                         out_specs=(act, act, P(("pod", "data"), None)), check_vma=False)
```

time: 639 us -> 91.8 us (0.14); the launches traced: 630 us -> 91.6 us
  waiting for transfers between devices: 400 us -> 0 us
  matrix products: 90.7 us -> 0 us
  local copies, waits for them, and re-layouts: 93.4 us -> 3.34 us
  Pallas kernels: 0 us -> 87.7 us
  other arithmetic: 25.2 us -> 0 us
  between operations: 14.7 us -> 0.64 us
    reduce_scatter x1 -> x0, waiting for transfers between devices: 337 us -> none  [local_layer(): lax.psum_scatter(dw_local, 'data', scatter_dimension=0, tiled=True)]
    dot_general x24 -> x0, matrix products: 90.7 us -> none  [the longest x1 7.89 us: local_layer(): jnp.einsum('nhts,nshk->nthk', dv_scores, k_feat, preferred_element_type=j...]
    pallas_call x0 -> x1, Pallas kernels: none -> 87.7 us  [local(): pl.pallas_call(lambda *refs: kernel(scale, *refs), out_shape=(vm((TOK, DI...]
    psum x1 -> x0, waiting for transfers between devices: 63.2 us -> none  [local_layer(): dw_part = lax.psum(dw_part, 'seq')]
    reshape x8 -> x0, local copies, waits for them, and re-layouts: 49.2 us -> none  [the longest x2 12.5 us: local_layer(): k_feat = jax.nn.silu(k_pre).astype(jnp.bfloat16).reshape(heads_shape)]
    mul x4 -> x0, local copies, waits for them, and re-layouts: 29.6 us -> none  [the longest x2 14.8 us: local_layer(): attn_scale * dq_val.reshape(flat_shape) * silu_grad(q_pre)]
    convert_element_type x2 -> x0, other arithmetic: 10.6 us -> none  [the longest x1 5.66 us: local_layer(): (attn_scale * dk_val.reshape(flat_shape) * silu_grad(k_pre)).astype(jnp.b...]
    unnamed x53 -> x3, local copies, waits for them, and re-layouts: 11.1 us -> 3.34 us
  transfers between devices with their start and end apart: 4 -> 0, of which waited for: 2 -> 0; matrix products, arithmetic and copies ran while one was open for 9% -> 0% of each run, Pallas kernels for 0% -> 0%
where the time goes in v2:
time: 91.8 us; the launch traced here: 91.6 us
  Pallas kernels  87.7 us (96%)
  local copies, waits for them, and re-layouts  3.34 us (4%)
    pallas_call x1, Pallas kernels, local(): pl.pallas_call(lambda *refs: kernel(scale, *refs), out_shape=(vm((TOK, DI...  87.7 us
    unnamed x3, local copies, waits for them, and re-layouts  3.34 us

profile of v2, /device:TPU:1, one launch (start us, length us, event | category | flops | bytes accessed | tf_op | source)
XLA Modules:
  0.0 91.6 jit_solution(7009895802405116801)
XLA Ops:
  0.6 87.7 %layer.1 = (bf16[1024,1024]{1,0:T(8,128)(2,1)S(1)}, bf16[1024,1024]{1,0:T(8,128)(2,1)S(1)}, f32[64,1024]{1,0:T(8,128)S(1)}) custom-call(bf16[1024,1024]{1,0:T(8,128)(2,1)} %bitcast.7, bf16[1024,1024]{1,0:T(8,128)(2,1)} %bitcast.8, bf16[1024,1024]{1,0:T(8,128)(2,1)} %refs_2_.1, bf16[1024,1024]{1,0:T(8,128)(2,1)} %refs_3_.1, bf16[1024,1024]{1,0:T(8,128)(2,1)} %refs_4_.1, ...), custom_call_target="tpu_custom_call" | custom-call | tf_op jit(solution)/shard_map/layer/pallas_call | solution.py:528
  88.3 1.3 %copy.12 = bf16[1,1024,1024]{2,1,0:T(8,128)(2,1)} copy(bf16[1,1024,1024]{2,1,0:T(8,128)(2,1)S(1)} %bitcast.6) | data formatting | bytes 4194304
  89.6 1.3 %copy.13 = bf16[1,1024,1024]{2,1,0:T(8,128)(2,1)} copy(bf16[1,1024,1024]{2,1,0:T(8,128)(2,1)S(1)} %bitcast.5) | data formatting | bytes 4194304
  90.9 0.7 copy.14

commit v3 on v2

--- a/solution.py
+++ b/solution.py
@@ -242,8 +242,25 @@
     lanes = lax.broadcasted_iota(jnp.int32, (1, 128), 1)
     first = (lanes < 64).astype(F32).astype(BF16)
     second = (lanes >= 64).astype(F32).astype(BF16)
-    causal = (lax.broadcasted_iota(jnp.int32, (CHUNK, CHUNK), 0)
-              >= lax.broadcasted_iota(jnp.int32, (CHUNK, CHUNK), 1))
+    tri = (lax.broadcasted_iota(jnp.int32, (128, 256), 0)
+           >= lax.rem(lax.broadcasted_iota(jnp.int32, (128, 256), 1), 128))
+
+    def stacked(a, n):
+        part = a[n * 128:n * 128 + 128]
+        return jnp.concatenate([part * first, part * second], axis=0)
+
+    def masked(sc):
+        top = jnp.where(tri, sc[:128], 0.0).astype(BF16)
+        return top if sc.shape[0] == 128 else jnp.concatenate([top, sc[128:].astype(BF16)], axis=0)
+
+    def lower(full, extra):
+        return jnp.concatenate([full[:128], full[128:] + extra], axis=0)
+
+    def turned(s0, s1, r):
+        wide = t_dot(s0, r)
+        tail = jnp.concatenate([s1[:, :128].T, s1[:, 128:].T], axis=1)
+        return jnp.concatenate([jnp.where(lanes < 64, wide[:128], wide[128:]), dot(tail, stacked(r, 1))], axis=0)
+
     block_diag = ((lax.broadcasted_iota(jnp.int32, (128, 128), 0) < 64)
                   == (lax.broadcasted_iota(jnp.int32, (128, 128), 1) < 64))
 
@@ -297,19 +314,16 @@
                 ocols = pl.ds(g * GRP + j * 128, 128)
                 q, k, v = qg[rows, cols], kg[rows, cols], vg[rows, cols]
                 do = dx_ref[drows, pl.ds(pl.multiple_of(lax.div(i, 4) * GRP + j * 128, 128), 128)]
-                qa, qb, ka, kb = q * first, q * second, k * first, k * second
-                va, vb, da, db = v * first, v * second, do * first, do * second
-                p_a = jnp.where(causal, dot_t(qa, k), 0.0).astype(BF16)
-                p_b = jnp.where(causal, dot_t(qb, k), 0.0).astype(BF16)
-                d_a = jnp.where(causal, dot_t(da, v), 0.0).astype(BF16)
-                d_b = jnp.where(causal, dot_t(db, v), 0.0).astype(BF16)
-                o = dot(p_a, va) + dot(p_b, vb) + dot(q, pre)
+                k0, k1, v0, v1 = stacked(k, 0), stacked(k, 1), stacked(v, 0), stacked(v, 1)
+                p0, p1 = masked(dot_t(q, k0)), masked(dot_t(q[128:], k1))
+                d0, d1 = masked(dot_t(do, v0)), masked(dot_t(do[128:], v1))
+                o = lower(dot(p0, v0) + dot(q, pre), dot(p1, v1))
                 oo[rows, ocols] = (scale * o).astype(BF16)
-                dq = dot(d_a, ka) + dot(d_b, kb) + dot_t(do, pre)
+                dq = lower(dot(d0, k0) + dot_t(do, pre), dot(d1, k1))
                 gq[rows, ocols] = (scale * dq * sga[rows, cols]).astype(BF16)
-                dk = t_dot(d_a, qa) + t_dot(d_b, qb) + dot_t(v, suf)
+                dk = dot_t(v, suf) + turned(d0, d1, q)
                 gk[rows, ocols] = (scale * dk * sgb[rows, cols]).astype(BF16)
-                dv = t_dot(p_a, da) + t_dot(p_b, db) + dot(k, suf)
+                dv = dot(k, suf) + turned(p0, p1, do)
                 gv[rows, ocols] = (scale * dv).astype(BF16)
             return 0
 
@@ -505,6 +519,18 @@
     return [pltpu.VMEM((2, 2) + (4,) * rest + (PART_ROWS[part][1], 128), F32)] * 3
 
 
+def write_out(y_in, dx_in, dw_in, y_out, dx_out, dw_out, sems):
+    copies = [pltpu.make_async_copy(dw_in, dw_out, sems.at[8])]
+    for n in range(4):
+        rows = pl.ds(n * (TOK // 4), TOK // 4)
+        copies.append(pltpu.make_async_copy(y_in.at[rows], y_out.at[rows], sems.at[n]))
+        copies.append(pltpu.make_async_copy(dx_in.at[rows], dx_out.at[rows], sems.at[4 + n]))
+    for c in copies:
+        c.start()
+    for c in copies:
+        c.wait()
+
+
 def solution(mesh):
     act = P(("pod", "data"), "seq", None)
     scale = float((64 * SEQ) ** -0.5)
@@ -525,7 +551,7 @@
                 scratch += hop_shapes(part, phase)
         scratch += [pltpu.SemaphoreType.DMA((NUM_SEMS,)), pltpu.SemaphoreType.DMA((NUM_SEMS,)),
                     pltpu.SemaphoreType.DMA((NUM_LOCAL,))]
-        y, dx, dw = pl.pallas_call(
+        held = pl.pallas_call(
             lambda *refs: kernel(scale, *refs),
             out_shape=(vm((TOK, DIM), BF16), vm((TOK, DIM), BF16), vm((ROWS, DIM), F32)),
             in_specs=[any_] * 6,
@@ -534,6 +560,16 @@
             name="layer",
             compiler_params=pltpu.CompilerParams(collective_id=0, has_side_effects=True, vmem_limit_bytes=62560000),
         )(x[0], dy[0], wq, wk, wv, wo.reshape(DIM, DIM))
+        y, dx, dw = pl.pallas_call(
+            write_out,
+            out_shape=(jax.ShapeDtypeStruct((TOK, DIM), BF16), jax.ShapeDtypeStruct((TOK, DIM), BF16),
+                       jax.ShapeDtypeStruct((ROWS, DIM), F32)),
+            in_specs=[pl.BlockSpec(memory_space=pltpu.VMEM)] * 3,
+            out_specs=(any_,) * 3,
+            scratch_shapes=[pltpu.SemaphoreType.DMA((9,))],
+            name="write_out",
+            compiler_params=pltpu.CompilerParams(vmem_limit_bytes=16 * 1024 * 1024),
+        )(*held)
         return y[None], dx[None], dw
 
     return jax.shard_map(local, mesh=mesh,

time: 91.8 us -> 89.2 us (0.972)
  local copies, waits for them, and re-layouts: 3.34 us -> 0 us
    unnamed x3 -> x0, local copies, waits for them, and re-layouts: 3.34 us -> none
    pallas_call x0 -> x1, Pallas kernels: none -> 2.17 us  [local(): pl.pallas_call(write_out, out_shape=(jax.ShapeDtypeStruct((TOK, DIM), BF1...]
    pallas_call x1, Pallas kernels: 87.7 us -> 86.1 us  [local(): pl.pallas_call(lambda *refs: kernel(scale, *refs), out_shape=(vm((TOK, DI...]
where the time goes in v3:
time: 89.2 us; the launch traced here: 89.1 us
  Pallas kernels  88.3 us (99%)
    pallas_call x1, Pallas kernels, local(): pl.pallas_call(lambda *refs: kernel(scale, *refs), out_shape=(vm((TOK, DI...  86.1 us
    pallas_call x1, Pallas kernels, local(): pl.pallas_call(write_out, out_shape=(jax.ShapeDtypeStruct((TOK, DIM), BF1...  2.17 us

profile of v3, /device:TPU:1, one launch (start us, length us, event | category | flops | bytes accessed | tf_op | source)
XLA Modules:
  0.0 89.1 jit_solution(6410819734357095817)
XLA Ops:
  0.6 86.1 %layer.1 = (bf16[1024,1024]{1,0:T(8,128)(2,1)S(1)}, bf16[1024,1024]{1,0:T(8,128)(2,1)S(1)}, f32[64,1024]{1,0:T(8,128)S(1)}) custom-call(bf16[1024,1024]{1,0:T(8,128)(2,1)} %bitcast.5, bf16[1024,1024]{1,0:T(8,128)(2,1)} %bitcast.6, bf16[1024,1024]{1,0:T(8,128)(2,1)} %refs_2_.1, bf16[1024,1024]{1,0:T(8,128)(2,1)} %refs_3_.1, bf16[1024,1024]{1,0:T(8,128)(2,1)} %refs_4_.1, ...), custom_call_target="tpu_custom_call" | custom-call | tf_op jit(solution)/shard_map/layer/pallas_call | solution.py:554
  86.8 2.2 %write_out.1 = (bf16[1024,1024]{1,0:T(8,128)(2,1)}, bf16[1024,1024]{1,0:T(8,128)(2,1)}, f32[64,1024]{1,0:T(8,128)}) custom-call(bf16[1024,1024]{1,0:T(8,128)(2,1)S(1)} %get-tuple-element.9.y_in, bf16[1024,1024]{1,0:T(8,128)(2,1)S(1)} %get-tuple-element.10.dx_in, f32[64,1024]{1,0:T(8,128)S(1)} %get-tuple-element.11.dw_in), custom_call_target="tpu_custom_call" | custom-call | tf_op jit(solution)/shard_map/write_out/pallas_call | solution.py:563

commit v4 on v3

--- a/solution.py
+++ b/solution.py
@@ -37,7 +37,7 @@
 
 
 NUM_SEMS = 240
-NUM_LOCAL = 12
+NUM_LOCAL = 14
 KINDS = {"1A": (0, 2, 0, 1), "1B": (1, 2, 0, -1), "RB": (1, 1, 1, 1), "LA": (0, 3, 2, -1),
          "RA": (0, 1, 1, 1), "LB": (1, 3, 2, -1),
          "O": (slice(None), 2, 0, 2), "R": (slice(None), 1, 1, 1), "L": (slice(None), 3, 2, -1)}
@@ -233,9 +233,10 @@
         loads[name] = pltpu.make_async_copy(src, dst, local_sem.at[len(loads)])
         loads[name].start()
 
-    load("x", x_hbm, xf.at[pl.ds(own0, TOK)])
+    load("x0", x_hbm.at[pl.ds(0, BLK)], xf.at[pl.ds(own0, BLK)])
     for name, src, dst in (("wq", wq_hbm, wq), ("wk", wk_hbm, wk), ("wv", wv_hbm, wv)):
         load(name, src.at[:, own_c], dst)
+    load("x1", x_hbm.at[pl.ds(BLK, BLK)], xf.at[pl.ds(own0 + BLK, BLK)])
     load("dy", dy_hbm, dyf.at[pl.ds(own0, TOK)])
     load("wo", wo_hbm.at[own_c], wo)
 
@@ -272,22 +273,26 @@
                 cs = slice(j * 128, j * 128 + 128)
                 raw[lax.div(base, CHUNK) + n, j] = p[cs, cs]
 
-    def project_x(g, base, blk):
+    def project_x(g, base, blk, ready=lambda name: None):
         rows = pl.ds(base, blk)
         gcols = pl.ds(g * GRP, GRP)
         xa = xf[rows, :]
+        pre_act = []
+        for name, w in (("wq", wq), ("wk", wk)):
+            ready(name)
+            pre_act.append(dot(xa, w[:, gcols]))
+        ready("wv")
+        v = dot(xa, wv[:, gcols]).astype(BF16)
+        vg[rows, :] = v
+        for a, sg, out in ((pre_act[0], sga, qg), (pre_act[1], sgb, kg)):
+            s = pl.reciprocal(1.0 + jnp.exp2(a * -1.4426950408889634))
+            f = a * s
+            kept = f.astype(BF16)
+            out[rows, :] = kept
+            sg[rows, :] = s + f * (1.0 - s)
         if g == 0:
             xt[:, rows] = xa.T
-        kept = []
-        for w, sg, out in ((wq, sga, qg), (wk, sgb, kg)):
-            a = dot(xa, w[:, gcols])
-            s = pl.reciprocal(1.0 + jnp.exp(-a))
-            kept.append((a * s).astype(BF16))
-            out[rows, :] = kept[-1]
-            sg[rows, :] = s * (1.0 + a * (1.0 - s))
-        v = dot(xa, wv[:, gcols]).astype(BF16)
-        vg[rows, :] = v
-        chunk_products(kept[1], v, kv_raw, base, blk)
+        chunk_products(kept, v, kv_raw, base, blk)
 
     def project_dy(g, half, base):
         rows = pl.ds(base, TOK)
@@ -361,17 +366,17 @@
         return o_copy, g_copies
 
     a0 = core * TOK
-    with jax.named_scope("load0"):
-        for name in ("x", "wq", "wk", "wv"):
-            loads[name].wait()
-    project_x(0, pl.multiple_of(a0, BLK), BLK)
     with jax.named_scope("barrier"):
         pl.semaphore_wait(barrier, 7)
     x_send = remote("x", x_hbm, xf.at[pl.ds(own0, TOK)], partner)
     dy_send = remote("dy", dy_hbm, dyf.at[pl.ds(own0, TOK)], partner)
     start(x_send)
     start(dy_send)
+    with jax.named_scope("load0"):
+        loads["x0"].wait()
+    project_x(0, pl.multiple_of(a0, BLK), BLK, lambda name: loads[name].wait())
     with jax.named_scope("projA0"):
+        loads["x1"].wait()
         project_x(0, pl.multiple_of(a0 + BLK, BLK), BLK)
         for name in ("dy", "wo"):
             loads[name].wait()
@@ -423,23 +428,18 @@
     with jax.named_scope("scan1"):
         scan_states()
     with jax.named_scope("attend1a"):
-        attend(1, 0, 3)
+        attend(1, 0, 4)
     with jax.named_scope("f1_0"):
         finish(("E0", "L0"), 0)
     with jax.named_scope("attend1b"):
-        attend(1, 3, 7)
+        attend(1, 4, 8)
+    o_copy1, g_copies1 = share(1)
     with jax.named_scope("r2_0"):
         relay(("E0", "L0"), 1)
-    with jax.named_scope("attend1c"):
-        attend(1, 7, 8)
-    o_copy1, g_copies1 = share(1)
     with jax.named_scope("wgrad1"):
         for m in range(3):
             weight_grad(1, m)
             ring_start("E1", ("1A", "1B"), m)
-            if m == 1:
-                with jax.named_scope("f2_0"):
-                    finish(("E0", "L0"), 1)
     with jax.named_scope("dwo1"):
         o_copy1.wait_recv()
         out_weight_grad(1)
@@ -447,6 +447,8 @@
         for m in range(3):
             ring_start("E1", ("RB", "LA"), m)
         ring_start("L1", ("RB", "LA"))
+    with jax.named_scope("f2_0"):
+        finish(("E0", "L0"), 1)
 
     def y_part(r, n):
         rows, cols = pl.ds(pl.multiple_of(own0 + r * HALF, HALF), HALF), pl.ds(n * HALF, HALF)
@@ -476,10 +478,10 @@
         relay(("E1", "L1"), 0)
     with jax.named_scope("dX1"):
         dx_part(0, 1)
+    with jax.named_scope("dX2"):
+        dx_part(1, 0)
     with jax.named_scope("f3_0"):
         finish(("E0", "L0"), 2)
-    with jax.named_scope("dX2"):
-        dx_part(1, 0)
     with jax.named_scope("dX3"):
         dx_part(1, 1)
     last_gens = ("E1", "L1")

time: 89.2 us -> 87.1 us (0.976)
  Pallas kernels: 88.3 us -> 86.2 us
    pallas_call x1, Pallas kernels: 86.1 us -> 84 us  [local(): pl.pallas_call(lambda *refs: kernel(scale, *refs), out_shape=(vm((TOK, DI...]
where the time goes in v4:
time: 87.1 us; the launch traced here: 87 us
  Pallas kernels  86.2 us (99%)
    pallas_call x1, Pallas kernels, local(): pl.pallas_call(lambda *refs: kernel(scale, *refs), out_shape=(vm((TOK, DI...  84 us
    pallas_call x1, Pallas kernels, local(): pl.pallas_call(write_out, out_shape=(jax.ShapeDtypeStruct((TOK, DIM), BF1...  2.17 us

profile of v4, /device:TPU:1, one launch (start us, length us, event | category | flops | bytes accessed | tf_op | source)
XLA Modules:
  0.0 87.0 jit_solution(7767232378169009048)
XLA Ops:
  0.6 84.0 %layer.1 = (bf16[1024,1024]{1,0:T(8,128)(2,1)S(1)}, bf16[1024,1024]{1,0:T(8,128)(2,1)S(1)}, f32[64,1024]{1,0:T(8,128)S(1)}) custom-call(bf16[1024,1024]{1,0:T(8,128)(2,1)} %bitcast.5, bf16[1024,1024]{1,0:T(8,128)(2,1)} %bitcast.6, bf16[1024,1024]{1,0:T(8,128)(2,1)} %refs_2_.1, bf16[1024,1024]{1,0:T(8,128)(2,1)} %refs_3_.1, bf16[1024,1024]{1,0:T(8,128)(2,1)} %refs_4_.1, ...), custom_call_target="tpu_custom_call" | custom-call | tf_op jit(solution)/shard_map/layer/pallas_call | solution.py:556
  84.6 2.2 %write_out.1 = (bf16[1024,1024]{1,0:T(8,128)(2,1)}, bf16[1024,1024]{1,0:T(8,128)(2,1)}, f32[64,1024]{1,0:T(8,128)}) custom-call(bf16[1024,1024]{1,0:T(8,128)(2,1)S(1)} %get-tuple-element.9.y_in, bf16[1024,1024]{1,0:T(8,128)(2,1)S(1)} %get-tuple-element.10.dx_in, f32[64,1024]{1,0:T(8,128)S(1)} %get-tuple-element.11.dw_in), custom_call_target="tpu_custom_call" | custom-call | tf_op jit(solution)/shard_map/write_out/pallas_call | solution.py:565

commit v5 on v4

--- a/solution.py
+++ b/solution.py
@@ -332,7 +332,7 @@
                 gv[rows, ocols] = (scale * dv).astype(BF16)
             return 0
 
-        lax.fori_loop(lo, hi, body, 0)
+        lax.fori_loop(lo, hi, body, 0, unroll=2)
 
     def weight_grad(g, m):
         gr = (gq, gk, gv)[m]
@@ -413,13 +413,12 @@
         project_dy(1, core, own0)
     with jax.named_scope("r1E0"):
         relay(("E0",), 0)
-    with jax.named_scope("projB1a"):
+    with jax.named_scope("projB1"):
         for n in range(2):
             project_x(1, pl.multiple_of(oth0 + n * BLK, BLK), BLK)
+        project_dy(1, other, oth0)
     with jax.named_scope("r1L0"):
         relay(("L0",), 0)
-    with jax.named_scope("projB1b"):
-        project_dy(1, other, oth0)
     load("wq2", wq_hbm.at[:, oth_c], xf.at[pl.ds(0, DIM), pl.ds(0, HALF)])
     load("wk2", wk_hbm.at[:, oth_c], xf.at[pl.ds(0, DIM), pl.ds(HALF, HALF)])
     load("wv2", wv_hbm.at[:, oth_c], xf.at[pl.ds(DIM, DIM), pl.ds(0, HALF)])
@@ -440,12 +439,13 @@
         for m in range(3):
             weight_grad(1, m)
             ring_start("E1", ("1A", "1B"), m)
+            if m:
+                ring_start("E1", ("RB", "LA"), m - 1)
     with jax.named_scope("dwo1"):
         o_copy1.wait_recv()
         out_weight_grad(1)
         ring_start("L1", ("1A", "1B"))
-        for m in range(3):
-            ring_start("E1", ("RB", "LA"), m)
+        ring_start("E1", ("RB", "LA"), 2)
         ring_start("L1", ("RB", "LA"))
     with jax.named_scope("f2_0"):
         finish(("E0", "L0"), 1)

time: 87.1 us -> 85.6 us (0.983)
  Pallas kernels: 86.2 us -> 84.6 us
    pallas_call x1, Pallas kernels: 84 us -> 82.5 us  [local(): pl.pallas_call(lambda *refs: kernel(scale, *refs), out_shape=(vm((TOK, DI...]
where the time goes in v5:
time: 85.6 us; the launch traced here: 85.5 us
  Pallas kernels  84.6 us (99%)
    pallas_call x1, Pallas kernels, local(): pl.pallas_call(lambda *refs: kernel(scale, *refs), out_shape=(vm((TOK, DI...  82.5 us
    pallas_call x1, Pallas kernels, local(): pl.pallas_call(write_out, out_shape=(jax.ShapeDtypeStruct((TOK, DIM), BF1...  2.17 us

profile of v5, /device:TPU:1, one launch (start us, length us, event | category | flops | bytes accessed | tf_op | source)
XLA Modules:
  0.0 85.5 jit_solution(14459105804856826990)
XLA Ops:
  0.6 82.5 %layer.1 = (bf16[1024,1024]{1,0:T(8,128)(2,1)S(1)}, bf16[1024,1024]{1,0:T(8,128)(2,1)S(1)}, f32[64,1024]{1,0:T(8,128)S(1)}) custom-call(bf16[1024,1024]{1,0:T(8,128)(2,1)} %bitcast.5, bf16[1024,1024]{1,0:T(8,128)(2,1)} %bitcast.6, bf16[1024,1024]{1,0:T(8,128)(2,1)} %refs_2_.1, bf16[1024,1024]{1,0:T(8,128)(2,1)} %refs_3_.1, bf16[1024,1024]{1,0:T(8,128)(2,1)} %refs_4_.1, ...), custom_call_target="tpu_custom_call" | custom-call | tf_op jit(solution)/shard_map/layer/pallas_call | solution.py:556
  83.1 2.2 %write_out.1 = (bf16[1024,1024]{1,0:T(8,128)(2,1)}, bf16[1024,1024]{1,0:T(8,128)(2,1)}, f32[64,1024]{1,0:T(8,128)}) custom-call(bf16[1024,1024]{1,0:T(8,128)(2,1)S(1)} %get-tuple-element.9.y_in, bf16[1024,1024]{1,0:T(8,128)(2,1)S(1)} %get-tuple-element.10.dx_in, f32[64,1024]{1,0:T(8,128)S(1)} %get-tuple-element.11.dw_in), custom_call_target="tpu_custom_call" | custom-call | tf_op jit(solution)/shard_map/write_out/pallas_call | solution.py:565

commit v6 on v5

--- a/solution.py
+++ b/solution.py
@@ -482,19 +482,21 @@
         dx_part(1, 0)
     with jax.named_scope("f3_0"):
         finish(("E0", "L0"), 2)
+    last_gens = ("E1", "L1")
+    with jax.named_scope("f1_1z"):
+        finish(last_gens, 0, (0,))
     with jax.named_scope("dX3"):
         dx_part(1, 1)
-    last_gens = ("E1", "L1")
     with jax.named_scope("f1_1"):
-        finish(last_gens, 0)
+        finish(last_gens, 0, (1, 2))
     with jax.named_scope("sends"):
         early = sent[:-36]
         del sent[:-36]
         wait_sends(early)
     with jax.named_scope("r2_1"):
-        relay(last_gens, 1)
+        relay(last_gens, 1, (0, 1, 2))
     with jax.named_scope("f2_1"):
-        finish(last_gens, 1)
+        finish(last_gens, 1, (0, 1, 2))
     with jax.named_scope("f3_1"):
         finish(last_gens, 2)
 

time: 85.6 us -> 85.6 us (level)
  no operation moved by 1% of the time
where the time goes in v6:
time: 85.6 us; the launch traced here: 85.5 us
  Pallas kernels  84.7 us (99%)
    pallas_call x1, Pallas kernels, local(): pl.pallas_call(lambda *refs: kernel(scale, *refs), out_shape=(vm((TOK, DI...  82.5 us
    pallas_call x1, Pallas kernels, local(): pl.pallas_call(write_out, out_shape=(jax.ShapeDtypeStruct((TOK, DIM), BF1...  2.17 us

profile of v6, /device:TPU:1, one launch (start us, length us, event | category | flops | bytes accessed | tf_op | source)
XLA Modules:
  0.0 85.5 jit_solution(15188700811531079340)
XLA Ops:
  0.6 82.5 %layer.1 = (bf16[1024,1024]{1,0:T(8,128)(2,1)S(1)}, bf16[1024,1024]{1,0:T(8,128)(2,1)S(1)}, f32[64,1024]{1,0:T(8,128)S(1)}) custom-call(bf16[1024,1024]{1,0:T(8,128)(2,1)} %bitcast.5, bf16[1024,1024]{1,0:T(8,128)(2,1)} %bitcast.6, bf16[1024,1024]{1,0:T(8,128)(2,1)} %refs_2_.1, bf16[1024,1024]{1,0:T(8,128)(2,1)} %refs_3_.1, bf16[1024,1024]{1,0:T(8,128)(2,1)} %refs_4_.1, ...), custom_call_target="tpu_custom_call" | custom-call | tf_op jit(solution)/shard_map/layer/pallas_call | solution.py:558
  83.1 2.2 %write_out.1 = (bf16[1024,1024]{1,0:T(8,128)(2,1)}, bf16[1024,1024]{1,0:T(8,128)(2,1)}, f32[64,1024]{1,0:T(8,128)}) custom-call(bf16[1024,1024]{1,0:T(8,128)(2,1)S(1)} %get-tuple-element.9.y_in, bf16[1024,1024]{1,0:T(8,128)(2,1)S(1)} %get-tuple-element.10.dx_in, f32[64,1024]{1,0:T(8,128)S(1)} %get-tuple-element.11.dw_in), custom_call_target="tpu_custom_call" | custom-call | tf_op jit(solution)/shard_map/write_out/pallas_call | solution.py:567
